TPU v7x, 128 devices: a whole 4x4x4 slice. The times are simulated.
128 devices in a mesh: row: 8 (over z, y_hi), col: 16 (over y_lo, x, core).
Axes of the slice: x: 4, y: 4 (y_hi: 2, y_lo: 2; y = y_hi * 2 + y_lo), z: 4, core: 2. Of those that a mesh axis runs over, the one named last changes fastest.
Arguments:
- matrix: float32 [16, 1024, 8, 2048], P(None, 'row', None, 'col'), may hold values from -150 to 150
- inverse_rest: float32 [16, 1024, 7, 2048], P(None, 'row', None, 'col'), may hold values from -6 to 6
- upper_block: float32 [2, 1024, 1, 2048], P(None, 'row', None, 'col'), may hold values from -6 to 6, as said below
- lower_below: float32 [2, 1024, 7, 2048], P(None, 'row', None, 'col'), may hold values from -0.046875 to 0.046875
- lower_inverse: float32 [2, 1024, 2048], P(None, 'row', 'col'), may hold values from -1 to 1, as said below
Outputs:
- plus_rows: float32 [2, 1024, 8, 2048], P(None, 'row', None, 'col')
Inputs may be any that keep to these rules, and one draw needn't show every extreme that they name: `upper_block`: upper triangular. `lower_inverse`: unit lower triangular.
All inputs are finite; a program needn't handle non-finite values.
Results may differ from a plain program's by a relative error of at most 0.000052.
Values sent between devices are 32-bit elements; how exact they have to be, the bound alone decides.
A program may use at most 192 MiB of HBM per device.

v0:
```python
import jax
import jax.numpy as jnp
from jax import lax
from jax.sharding import Mesh
from jax.sharding import PartitionSpec as P

ROW = ("row_0", "row_1")
COL = ("col_0", "col_1", "col_2")
ROW_COL = ("row_0", "row_1", "col_0", "col_1", "col_2")


def over_axes(array, axes):
    for axis in axes:
        array = lax.psum(array, axis)
    return array


def laid_out(pieces, dim):
    lengths = list(pieces.shape[1:])
    lengths[dim] *= pieces.shape[0]
    return jnp.moveaxis(pieces, 0, dim).reshape(lengths)


def from_everyone(array, axis):
    count = lax.axis_size(axis)
    return lax.all_to_all(
        jnp.broadcast_to(array[None], (count, *array.shape)), axis, 0, 0, tiled=True
    )


def collect(array, axis, dim):
    return laid_out(from_everyone(array, axis), dim)


def dot_exact(left, right, form):
    return jnp.einsum(
        form, left, right, precision=lax.Precision.HIGHEST, preferred_element_type=jnp.float32
    )


def mirror(panel_rows, row_devices, col_devices, panel_cycles, blk_size):
    share_rows, col_ratio, width_all = panel_rows.shape
    sectioned = panel_rows.reshape(share_rows, col_ratio, 1, panel_cycles, row_devices, blk_size)
    sectioned = lax.all_to_all(sectioned, ROW, split_axis=4, concat_axis=2, tiled=True)
    sectioned = sectioned.reshape(share_rows, col_devices, panel_cycles, blk_size)
    sectioned = lax.all_to_all(sectioned, COL, split_axis=1, concat_axis=0, tiled=True)
    return sectioned.reshape(col_devices * share_rows, panel_cycles * blk_size)


def per_device(matrix, inverse_rest, upper_block, lower_below, lower_inverse):
    row_devices = lax.axis_size(ROW)
    col_devices = lax.axis_size(COL)
    col_ratio = col_devices // row_devices
    row_cycles, blk_size, col_cycles, blk_again = matrix.shape
    panel_cycles = lower_inverse.shape[0]
    width_all = lower_inverse.shape[2] * col_devices
    rest_local = inverse_rest.shape[2] * blk_size
    panel_col_cycles = upper_block.shape[2]
    local_rows = col_cycles * blk_size
    share_rows = local_rows // col_devices
    matrix_sq = jnp.sum(matrix * matrix)
    rest_sq = jnp.sum(inverse_rest * inverse_rest)
    matrix_total, rest_total = (over_axes(matrix_sq, ROW_COL), over_axes(rest_sq, ROW_COL))
    below_all = lax.all_gather(lower_below, ROW, axis=1, tiled=True).reshape(width_all, rest_local)
    inverse_rows = (
        inverse_rest.reshape(col_cycles, col_ratio, blk_size, rest_local)
        .transpose(0, 2, 1, 3)
        .reshape(local_rows, col_ratio, rest_local)
    )
    padded = jnp.concatenate(
        [
            upper_block,
            jnp.zeros(
                (row_cycles - panel_cycles, blk_size, panel_col_cycles, blk_size), jnp.float32
            ),
        ],
        axis=0,
    )
    upper_rows = (
        padded.reshape(col_cycles, col_ratio, blk_size, panel_col_cycles * blk_size)
        .transpose(0, 2, 1, 3)
        .reshape(local_rows, col_ratio, panel_col_cycles, 1, blk_size)
    )
    owner_mask = lax.broadcasted_iota(jnp.int32, (1, 1, 1, col_devices, 1), 3) == lax.axis_index(
        COL
    )
    spread = jnp.where(owner_mask, upper_rows, 0.0).reshape(
        share_rows * lax.axis_size(COL), col_ratio, width_all
    )
    panel_share = lax.psum_scatter(
        spread - dot_exact(inverse_rows, below_all, "usm,tm->ust"),
        COL,
        scatter_dimension=0,
        tiled=True,
    )
    factor_rows = collect(lower_inverse, ROW, 1)
    factor_all = lax.all_gather(factor_rows, COL, axis=2, tiled=True).reshape(width_all, width_all)
    inverse_share = dot_exact(panel_share, factor_all, "ust,tw->usw")
    panel_sq = jnp.sum(inverse_share * inverse_share)
    mirrored = mirror(inverse_share, row_devices, col_devices, panel_cycles, blk_size)
    inverse_block = mirrored.reshape(col_cycles, blk_size, panel_cycles, blk_size).transpose(
        2, 3, 0, 1
    )
    panel_total = over_axes(panel_sq, ROW_COL)
    balance = jnp.sqrt(jnp.sqrt((rest_total + panel_total) / matrix_total))
    return 0.5 * (balance * matrix[:panel_cycles] + inverse_block / balance)


def solution(mesh):
    split = Mesh(mesh.devices.reshape(4, 2, 2, 4, 2), ("row_0", "row_1", "col_0", "col_1", "col_2"))
    return jax.shard_map(
        per_device,
        mesh=split,
        in_specs=(
            P(None, ROW, None, COL),
            P(None, ROW, None, COL),
            P(None, ROW, None, COL),
            P(None, ROW, None, COL),
            P(None, ROW, COL),
        ),
        out_specs=P(None, ROW, None, COL),
        check_vma=False,
    )
```

profile of v0, /device:TPU:1, one launch (start us, length us, event | category | flops | bytes accessed | tf_op | source)
XLA Modules:
  0.0 415.5 jit_solution(5951134886269617252)
XLA Ops:
  6.5 0.7 all-gather.3.cloned.1.call-update
  7.3 1.0 broadcast_in_dim.42
  8.3 27.6 %all_to_all.29 = f32[8,2,128,128]{3,2,1,0:T(8,128)S(1)} all-to-all(f32[8,2,128,128]{3,2,1,0:T(8,128)S(1)} %broadcast_in_dim.42), channel_id=1, replica_groups=mesh['row_0'=4,'row_1'=2,'col_0'=2,'col_1'=4,'col_2'=2] {'row_0','row_1'}, dimensions={0} | all-to-all | bytes 2097152 | tf_op jit(solution)/shard_map/all_to_all | solution.py:26
  35.9 1.1 copy.41
  37.0 1.0 concatenate.3
  38.2 6.8 %broadcast_in_dim.39 = f32[1024,2,16,128]{3,2,0,1:T(8,128)} broadcast(f32[1024,2,128]{2,0,1:T(8,128)S(1)} %bitcast.51), dimensions={0,1,3} | broadcast | bytes 17825792 | tf_op jit(solution)/shard_map/jit(_where)/broadcast_in_dim | solution.py:87
  45.0 18.1 %broadcast_in_dim.40 = f32[1024,2,2048]{2,0,1:T(8,128)} reshape(f32[1024,2,16,128]{3,2,0,1:T(8,128)} %broadcast_in_dim.39) | data formatting | bytes 33554432 | tf_op jit(solution)/shard_map/jit(_where)/broadcast_in_dim | solution.py:87
  63.1 8.6 %copy.37 = f32[16,128,7,128]{1,3,2,0:T(8,128)} copy(f32[16,128,7,128]{3,1,2,0:T(8,128)} %param.6) | data formatting | bytes 14680064 | tf_op args[1]
  71.7 8.1 %copy.38 = f32[8,128,2,896]{3,1,0,2:T(8,128)} copy(f32[8,128,2,896]{1,3,2,0:T(8,128)} %bitcast.48) | data formatting | bytes 14680064 | tf_op jit(solution)/shard_map/transpose | solution.py:67
  79.9 33.9 %all-gather.3.cloned.1.call-done = f32[2,1024,7,128]{3,1,2,0:T(8,128)} async-done(((f32[2,128,7,128]{3,1,2,0:T(8,128)}), f32[2,1024,7,128]{3,1,2,0:T(8,128)}) %all-gather.3.cloned.1.call-update) | async-done | bytes 7340048 | tf_op jit(solution)/shard_map/all_gather | solution.py:64
  113.8 11.8 %copy.39 = f32[2,1024,7,128]{1,0,3,2:T(2,128)} copy(f32[2,1024,7,128]{3,1,2,0:T(8,128)} %all-gather.3.cloned.1.call-done) | data formatting | bytes 14680064 | tf_op jit(solution)/shard_map/all_gather | solution.py:64
  125.6 10.7 %reshape.58 = f32[2048,896,1]{0,1,2:T(8,128)} reshape(f32[2,1024,7,128]{1,0,3,2:T(2,128)} %copy.39) | data formatting | bytes 14680064 | tf_op jit(solution)/shard_map/reshape | solution.py:64
  136.3 60.3 %select_subtract_fusion = f32[1024,2,2048]{2,0,1:T(8,128)} fusion(f32[1024,2,2048]{2,0,1:T(8,128)} %broadcast_in_dim.40, pred[2048]{0:T(1024)(128)(4,1)S(1)} %broadcast_bitcast_fusion, f32[1024,2,896]{2,0,1:T(8,128)} %bitcast.49, f32[2048,896,1]{0,1,2:T(8,128)} %reshape.58), kind=kOutput, calls=%fused_computation | convolution fusion | flops 45105545216 | bytes 48236544 | tf_op jit(solution)/shard_map/usm,tm->ust/dot_general | solution.py:36
  196.6 15.5 %all-gather.5.cloned.1.call-done = f32[2,1024,2048]{2,1,0:T(8,128)} async-done(((f32[2,1024,128]{2,1,0:T(8,128)}), f32[2,1024,2048]{2,1,0:T(8,128)}) %all-gather.5.cloned.1.call-update) | async-done | bytes 16777232 | tf_op jit(solution)/shard_map/all_gather | solution.py:97
  212.1 98.9 %reduce-scatter.2.cloned.1.call-done = f32[64,2,2048]{2,0,1:T(8,128)} async-done(((f32[1024,2,2048]{2,0,1:T(8,128)}), f32[64,2,2048]{2,0,1:T(8,128)}) %reduce-scatter.2.cloned.1.call-update) | async-done | bytes 1048592 | tf_op jit(solution)/shard_map/reduce_scatter | solution.py:90
  310.9 13.6 %multiply_reduce_fusion.2 = (f32[]{:T(128)}, f32[64,2,2048]{2,0,1:T(8,128)S(1)}) fusion(f32[64,2,2048]{2,0,1:T(8,128)} %reduce-scatter.2.cloned.1.call-done, f32[2048,2048,1]{1,0,2:T(8,128)} %bitcast.47), kind=kOutput, calls=%fused_computation.6 | convolution fusion | flops 6442975232 | bytes 18874372 | tf_op jit(solution)/shard_map/ust,tw->usw/dot_general | solution.py:36
  324.5 0.2 copy.51
  324.7 0.8 copy.43
  325.5 21.3 %all_to_all.30 = f32[64,2,1,2,8,128]{5,1,3,0,2,4:T(2,128)S(1)} all-to-all(f32[64,2,1,2,8,128]{5,1,3,0,2,4:T(2,128)S(1)} %copy.43), channel_id=1, replica_groups=mesh['row_0'=4,'row_1'=2,'col_0'=2,'col_1'=4,'col_2'=2] {'row_0','row_1'}, dimensions={4} | all-to-all | bytes 2097152 | tf_op jit(solution)/shard_map/all_to_all | solution.py:44
  346.8 0.6 copy.54
  347.5 1.5 copy.45
  349.0 7.3 %all-to-all-start.2 = ((f32[64,16,2,128]{3,2,0,1:T(2,128)}), f32[64,16,2,128]{3,2,0,1:T(2,128)S(1)}, u32[]{:S(2)}, u32[]{:S(2)}) async-start(f32[64,16,2,128]{3,2,0,1:T(2,128)} %copy.45), calls=%async_computation.3 | async-start | bytes 2097152 | tf_op jit(solution)/shard_map/all_to_all | solution.py:46
  356.3 5.7 %multiply_reduce_fusion.1 = f32[]{:T(128)} fusion(f32[16,128,7,128]{3,1,2,0:T(8,128)} %param.6), kind=kLoop, calls=%fused_computation.2 | loop fusion | flops 3670015 | bytes 7340036 | tf_op jit(solution)/shard_map/reduce_sum | solution.py:62
  361.9 6.2 %multiply_reduce_fusion = f32[]{:T(128)} fusion(f32[16,128,8,128]{3,2,1,0:T(8,128)} %param.5), kind=kLoop, calls=%fused_computation.1 | loop fusion | flops 4194303 | bytes 8388612 | tf_op jit(solution)/shard_map/reduce_sum | solution.py:61
  369.3 0.4 copy.50
  369.7 7.1 %all-reduce.2 = (f32[]{:T(128)}, f32[]{:T(128)}) all-reduce(f32[]{:T(128)S(6)} %add.48, f32[]{:T(128)} %multiply_reduce_fusion), channel_id=1, replica_groups=mesh['row_0'=4,'row_1'=2,'col_0'=2,'col_1'=4,'col_2'=2] {'row_0'}, use_global_device_ids=true, to_apply=%region_1.0 | all-reduce | flops 2 | bytes 16 | tf_op jit(solution)/shard_map/psum | solution.py:14
  376.7 5.9 %all-reduce.5 = (f32[]{:T(128)}, f32[]{:T(128)}) all-reduce(f32[]{:T(128)} %get-tuple-element.7, f32[]{:T(128)} %get-tuple-element.8), channel_id=1, replica_groups=mesh['row_0'=4,'row_1'=2,'col_0'=2,'col_1'=4,'col_2'=2] {'row_1'}, use_global_device_ids=true, to_apply=%region_2.0 | all-reduce | flops 2 | bytes 16 | tf_op jit(solution)/shard_map/psum | solution.py:14
  382.7 4.5 %all-reduce.4 = (f32[]{:T(128)}, f32[]{:T(128)}) all-reduce(f32[]{:T(128)} %get-tuple-element.13, f32[]{:T(128)} %get-tuple-element.14), channel_id=1, replica_groups=mesh['row_0'=4,'row_1'=2,'col_0'=2,'col_1'=4,'col_2'=2] {'col_0'}, use_global_device_ids=true, to_apply=%region_3.0 | all-reduce | flops 2 | bytes 16 | tf_op jit(solution)/shard_map/psum | solution.py:14
  387.1 9.2 %all-reduce.1 = (f32[]{:T(128)}, f32[]{:T(128)}) all-reduce(f32[]{:T(128)} %get-tuple-element.11, f32[]{:T(128)} %get-tuple-element.12), channel_id=1, replica_groups=mesh['row_0'=4,'row_1'=2,'col_0'=2,'col_1'=4,'col_2'=2] {'col_1'}, use_global_device_ids=true, to_apply=%region_4.0 | all-reduce | flops 2 | bytes 16 | tf_op jit(solution)/shard_map/psum | solution.py:14
  396.3 9.6 %all-reduce.3 = (f32[]{:T(128)}, f32[]{:T(128)}) all-reduce(f32[]{:T(128)} %get-tuple-element.5, f32[]{:T(128)} %get-tuple-element.6), channel_id=1, replica_groups=mesh['row_0'=4,'row_1'=2,'col_0'=2,'col_1'=4,'col_2'=2] {'col_2'}, use_global_device_ids=true, to_apply=%region_5.0 | all-reduce | flops 2 | bytes 16 | tf_op jit(solution)/shard_map/psum | solution.py:14
  407.5 0.1 add_multiply_fusion
  407.6 1.3 copy.47
  (12 shorter events, 0.4 us)
Async XLA Ops:
  6.5 107.3 %all-gather.3.cloned.1.call-start = ((), (), s32[]{:S(2)}) async-start(), calls=%async_computation.4 | async-start | bytes 8257536 | tf_op jit(solution)/shard_map/all_gather | solution.py:64
  7.3 204.8 %all-gather.5.cloned.1.call-start = ((), (), s32[]{:S(2)}) async-start(), calls=%async_computation.6 | async-start | bytes 17825792 | tf_op jit(solution)/shard_map/all_gather | solution.py:97
  37.0 273.9 %reduce-scatter.2.cloned.1.call-start = ((), (), s32[]{:S(2)}) async-start(), calls=%async_computation.5 | async-start | bytes 17825792 | tf_op jit(solution)/shard_map/reduce_scatter | solution.py:90
  349.0 58.4 %all-to-all-start.2 = ((f32[64,16,2,128]{3,2,0,1:T(2,128)}), f32[64,16,2,128]{3,2,0,1:T(2,128)S(1)}, u32[]{:S(2)}, u32[]{:S(2)}) async-start(f32[64,16,2,128]{3,2,0,1:T(2,128)} %copy.45), calls=%async_computation.3 | async-start | bytes 2097152 | tf_op jit(solution)/shard_map/all_to_all | solution.py:46
  356.3 13.0 %slice-start = ((f32[16,128,8,128]{3,2,1,0:T(8,128)}), f32[2,128,8,128]{3,2,1,0:T(8,128)S(1)}, s32[]{:S(2)}) async-start(f32[16,128,8,128]{3,2,1,0:T(8,128)} %param.5), calls=%async_computation.7 | async-start | bytes 2097152 | tf_op jit(solution)/shard_map/slice | solution.py:106
Sparse Core Ops, SparseCore 0:
  9.6 104.1 all-gather.2
  115.4 96.6 all-gather.4
  214.5 96.4 reduce-scatter.1
where the time goes:
time: 417 us; the launch traced here: 415 us
  waiting for transfers between devices  149 us (36%)
  blocking collectives  85.1 us (20%)
  matrix products  73.9 us (18%)
  local copies, waits for them, and re-layouts  72.2 us (17%)
  between operations  15.8 us (4%)
  other arithmetic  12.2 us (3%)
  starting transfers between devices  7.39 us (2%)
    reduce_scatter x1, waiting for transfers between devices, per_device(): lax.psum_scatter(spread - dot_exact(inverse_rows, below_all, 'usm,tm->ust...  98.9 us
    dot_general x2, matrix products, dot_exact(): jnp.einsum(form, left, right, precision=lax.Precision.HIGHEST, preferred_...  73.9 us
    psum x5, blocking collectives, over_axes(): array = lax.psum(array, axis)  36.2 us
    all_gather x1, waiting for transfers between devices, per_device(): lax.all_gather(lower_below, ROW, axis=1, tiled=True)  33.9 us
    all_to_all x1, blocking collectives, from_everyone(): lax.all_to_all(jnp.broadcast_to(array[None], (count, *array.shape)), axis...  27.6 us
    broadcast_in_dim x3, local copies, waits for them, and re-layouts, per_device(): jnp.where(owner_mask, upper_rows, 0.0)  25 us
    all_to_all x1, blocking collectives, mirror(): lax.all_to_all(sectioned, ROW, split_axis=4, concat_axis=2, tiled=True)  21.3 us
    all_gather x1, waiting for transfers between devices, per_device(): lax.all_gather(factor_rows, COL, axis=2, tiled=True)  15.5 us
  transfers between devices with their start and end apart: 4, of which 3 were waited for; matrix products, arithmetic and copies ran while one was open for 34% of the time, Pallas kernels for 0%

commit v1 on v0

--- a/solution.py
+++ b/solution.py
@@ -61,7 +61,9 @@
     matrix_sq = jnp.sum(matrix * matrix)
     rest_sq = jnp.sum(inverse_rest * inverse_rest)
     matrix_total, rest_total = (over_axes(matrix_sq, ROW_COL), over_axes(rest_sq, ROW_COL))
-    below_all = lax.all_gather(lower_below, ROW, axis=1, tiled=True).reshape(width_all, rest_local)
+    below_all = jnp.concatenate(
+        lax.all_to_all(jnp.stack([lower_below] * lax.axis_size(ROW)), ROW, 0, 0), axis=1
+    ).reshape(width_all, rest_local)
     inverse_rows = (
         inverse_rest.reshape(col_cycles, col_ratio, blk_size, rest_local)
         .transpose(0, 2, 1, 3)

time: 417 us -> 483 us (1.16)
  waiting for transfers between devices: 149 us -> 209 us
  starting transfers between devices: 7.39 us -> 12.3 us
    all_to_all x0 -> x1, waiting for transfers between devices: none -> 115 us  [per_device(): lax.all_to_all(jnp.stack([lower_below] * lax.axis_size(ROW)), ROW, 0, 0)]
    all_gather x1 -> x0, waiting for transfers between devices: 33.9 us -> none  [per_device(): lax.all_gather(lower_below, ROW, axis=1, tiled=True)]
    another operation x0 -> x2, local copies, waits for them, and re-layouts: none -> 15.5 us  [the longest x1 8.96 us: per_device(): below_all = jnp.concatenate(lax.all_to_all(jnp.stack([lower_below] * lax....]
    all_gather x1, waiting for transfers between devices: 15.5 us -> 0.02 us  [per_device(): lax.all_gather(factor_rows, COL, axis=2, tiled=True)]
    all_gather x1 -> x0, local copies, waits for them, and re-layouts: 11.8 us -> none  [per_device(): lax.all_gather(lower_below, ROW, axis=1, tiled=True)]
    all_to_all x0 -> x1, starting transfers between devices: none -> 5 us  [per_device(): lax.all_to_all(jnp.stack([lower_below] * lax.axis_size(ROW)), ROW, 0, 0)]
    unnamed x3 -> x6, local copies, waits for them, and re-layouts: 9.15 us -> 11 us
  transfers between devices with their start and end apart: 4 -> 4, of which waited for: 3 -> 2; matrix products, arithmetic and copies ran while one was open for 34% -> 29% of each run, Pallas kernels for 0% -> 0%
where the time goes in v1:
time: 483 us; the launch traced here: 482 us
  waiting for transfers between devices  209 us (43%)
  blocking collectives  82.2 us (17%)
  local copies, waits for them, and re-layouts  76.4 us (16%)
  matrix products  73.3 us (15%)
  between operations  16.2 us (3%)
  starting transfers between devices  12.3 us (3%)
  other arithmetic  12.2 us (3%)
    all_to_all x1, waiting for transfers between devices, per_device(): lax.all_to_all(jnp.stack([lower_below] * lax.axis_size(ROW)), ROW, 0, 0)  115 us
    reduce_scatter x1, waiting for transfers between devices, per_device(): lax.psum_scatter(spread - dot_exact(inverse_rows, below_all, 'usm,tm->ust...  94.1 us
    dot_general x2, matrix products, dot_exact(): jnp.einsum(form, left, right, precision=lax.Precision.HIGHEST, preferred_...  73.3 us
    psum x5, blocking collectives, over_axes(): array = lax.psum(array, axis)  36.3 us
    broadcast_in_dim x3, local copies, waits for them, and re-layouts, per_device(): jnp.where(owner_mask, upper_rows, 0.0)  24.9 us
    all_to_all x1, blocking collectives, from_everyone(): lax.all_to_all(jnp.broadcast_to(array[None], (count, *array.shape)), axis...  24.6 us
    all_to_all x1, blocking collectives, mirror(): lax.all_to_all(sectioned, ROW, split_axis=4, concat_axis=2, tiled=True)  21.3 us
    unnamed x6, local copies, waits for them, and re-layouts  11 us
  transfers between devices with their start and end apart: 4, of which 2 were waited for; matrix products, arithmetic and copies ran while one was open for 29% of the time, Pallas kernels for 0%

profile of v1, /device:TPU:1, one launch (start us, length us, event | category | flops | bytes accessed | tf_op | source)
XLA Modules:
  0.0 481.9 jit_solution(2821169025570760894)
XLA Ops:
  6.5 1.0 broadcast_in_dim.42
  7.5 24.6 %all_to_all.34 = f32[8,2,128,128]{3,2,1,0:T(8,128)S(1)} all-to-all(f32[8,2,128,128]{3,2,1,0:T(8,128)S(1)} %broadcast_in_dim.42), channel_id=1, replica_groups=mesh['row_0'=4,'row_1'=2,'col_0'=2,'col_1'=4,'col_2'=2] {'row_0','row_1'}, dimensions={0} | all-to-all | bytes 2097152 | tf_op jit(solution)/shard_map/all_to_all | solution.py:26
  32.2 1.1 copy.44
  33.3 1.9 copy.41
  35.1 6.5 %stack.2 = f32[8,2,128,7,128]{2,1,4,3,0:T(2,128)} broadcast(f32[2,128,7,128]{1,0,3,2:T(2,128)S(1)} %copy.41), dimensions={1,2,3,4} | broadcast | bytes 8257536 | tf_op jit(solution)/shard_map/stack | solution.py:65
  41.7 5.0 %all-to-all-start = ((f32[8,2,128,7,128]{2,1,4,3,0:T(2,128)}), f32[8,2,128,7,128]{2,1,4,3,0:T(2,128)}, u32[]{:S(2)}, u32[]{:S(2)}) async-start(f32[8,2,128,7,128]{2,1,4,3,0:T(2,128)} %stack.2), calls=%async_computation | async-start | bytes 14680064 | tf_op jit(solution)/shard_map/all_to_all | solution.py:65
  47.0 6.8 %broadcast_in_dim.39 = f32[1024,2,16,128]{3,2,0,1:T(8,128)} broadcast(f32[1024,2,128]{2,0,1:T(8,128)S(1)} %bitcast.54), dimensions={0,1,3} | broadcast | bytes 17825792 | tf_op jit(solution)/shard_map/jit(_where)/broadcast_in_dim | solution.py:89
  53.7 18.1 %broadcast_in_dim.40 = f32[1024,2,2048]{2,0,1:T(8,128)} reshape(f32[1024,2,16,128]{3,2,0,1:T(8,128)} %broadcast_in_dim.39) | data formatting | bytes 33554432 | tf_op jit(solution)/shard_map/jit(_where)/broadcast_in_dim | solution.py:89
  71.8 8.6 %copy.39 = f32[16,128,7,128]{1,3,2,0:T(8,128)} copy(f32[16,128,7,128]{3,1,2,0:T(8,128)} %param.6) | data formatting | bytes 14680064 | tf_op args[1]
  80.4 8.2 %copy.40 = f32[8,128,2,896]{3,1,0,2:T(8,128)} copy(f32[8,128,2,896]{1,3,2,0:T(8,128)} %bitcast.51) | data formatting | bytes 14680064 | tf_op jit(solution)/shard_map/transpose | solution.py:69
  88.7 115.1 %all-to-all-done = f32[8,2,128,7,128]{2,1,4,3,0:T(2,128)} async-done(((f32[8,2,128,7,128]{2,1,4,3,0:T(2,128)}), f32[8,2,128,7,128]{2,1,4,3,0:T(2,128)}, u32[]{:S(2)}, u32[]{:S(2)}) %all-to-all-start) | async-done | bytes 7340064 | tf_op jit(solution)/shard_map/all_to_all | solution.py:65
  203.8 10.2 %copy.42 = f32[2,8,128,7,128]{2,1,0,4,3:T(8,128)} copy(f32[2,8,128,7,128]{2,0,4,3,1:T(2,128)} %bitcast.8) | data formatting | bytes 14680064 | tf_op jit(solution)/shard_map/reshape | solution.py:64
  214.0 9.0 %reshape.60 = f32[2048,896,1]{0,1,2:T(8,128)} reshape(f32[2,8,128,7,128]{2,1,0,4,3:T(8,128)} %copy.42) | data formatting | bytes 14680064 | tf_op jit(solution)/shard_map/reshape;reshape | solution.py:66
  223.0 59.7 %select_subtract_fusion = f32[1024,2,2048]{2,0,1:T(8,128)} fusion(f32[1024,2,2048]{2,0,1:T(8,128)} %broadcast_in_dim.40, pred[2048]{0:T(1024)(128)(4,1)S(1)} %broadcast_bitcast_fusion, f32[1024,2,896]{2,0,1:T(8,128)} %bitcast.52, f32[2048,896,1]{0,1,2:T(8,128)} %reshape.60), kind=kOutput, calls=%fused_computation | convolution fusion | flops 45105545216 | bytes 48236544 | tf_op jit(solution)/shard_map/usm,tm->ust/dot_general | solution.py:36
  282.8 94.1 %reduce-scatter.2.cloned.1.call-done = f32[64,2,2048]{2,0,1:T(8,128)} async-done(((f32[1024,2,2048]{2,0,1:T(8,128)}), f32[64,2,2048]{2,0,1:T(8,128)}) %reduce-scatter.2.cloned.1.call-update) | async-done | bytes 1048592 | tf_op jit(solution)/shard_map/reduce_scatter | solution.py:92
  376.9 13.6 %multiply_reduce_fusion.2 = (f32[]{:T(128)}, f32[64,2,2048]{2,0,1:T(8,128)S(1)}) fusion(f32[64,2,2048]{2,0,1:T(8,128)} %reduce-scatter.2.cloned.1.call-done, f32[2048,2048,1]{1,0,2:T(8,128)} %bitcast.50), kind=kOutput, calls=%fused_computation.6 | convolution fusion | flops 6442975232 | bytes 18874372 | tf_op jit(solution)/shard_map/ust,tw->usw/dot_general | solution.py:36
  390.5 0.2 copy.54
  390.7 0.8 copy.46
  391.5 21.3 %all_to_all.35 = f32[64,2,1,2,8,128]{5,1,3,0,2,4:T(2,128)S(1)} all-to-all(f32[64,2,1,2,8,128]{5,1,3,0,2,4:T(2,128)S(1)} %copy.46), channel_id=1, replica_groups=mesh['row_0'=4,'row_1'=2,'col_0'=2,'col_1'=4,'col_2'=2] {'row_0','row_1'}, dimensions={4} | all-to-all | bytes 2097152 | tf_op jit(solution)/shard_map/all_to_all | solution.py:44
  412.8 0.6 copy.57
  413.4 1.5 copy.48
  414.9 7.3 %all-to-all-start.3 = ((f32[64,16,2,128]{3,2,0,1:T(2,128)}), f32[64,16,2,128]{3,2,0,1:T(2,128)S(1)}, u32[]{:S(2)}, u32[]{:S(2)}) async-start(f32[64,16,2,128]{3,2,0,1:T(2,128)} %copy.48), calls=%async_computation.4 | async-start | bytes 2097152 | tf_op jit(solution)/shard_map/all_to_all | solution.py:46
  422.3 5.7 %multiply_reduce_fusion.1 = f32[]{:T(128)} fusion(f32[16,128,7,128]{3,1,2,0:T(8,128)} %param.6), kind=kLoop, calls=%fused_computation.2 | loop fusion | flops 3670015 | bytes 7340036 | tf_op jit(solution)/shard_map/reduce_sum | solution.py:62
  428.0 6.2 %multiply_reduce_fusion = f32[]{:T(128)} fusion(f32[16,128,8,128]{3,2,1,0:T(8,128)} %param.5), kind=kLoop, calls=%fused_computation.1 | loop fusion | flops 4194303 | bytes 8388612 | tf_op jit(solution)/shard_map/reduce_sum | solution.py:61
  435.5 0.4 copy.53
  435.8 7.1 %all-reduce.2 = (f32[]{:T(128)}, f32[]{:T(128)}) all-reduce(f32[]{:T(128)S(6)} %add.48, f32[]{:T(128)} %multiply_reduce_fusion), channel_id=1, replica_groups=mesh['row_0'=4,'row_1'=2,'col_0'=2,'col_1'=4,'col_2'=2] {'row_0'}, use_global_device_ids=true, to_apply=%region_1.0 | all-reduce | flops 2 | bytes 16 | tf_op jit(solution)/shard_map/psum | solution.py:14
  442.9 6.0 %all-reduce.5 = (f32[]{:T(128)}, f32[]{:T(128)}) all-reduce(f32[]{:T(128)} %get-tuple-element.7, f32[]{:T(128)} %get-tuple-element.8), channel_id=1, replica_groups=mesh['row_0'=4,'row_1'=2,'col_0'=2,'col_1'=4,'col_2'=2] {'row_1'}, use_global_device_ids=true, to_apply=%region_2.0 | all-reduce | flops 2 | bytes 16 | tf_op jit(solution)/shard_map/psum | solution.py:14
  448.9 4.5 all-reduce.4
  453.3 9.2 %all-reduce.1 = (f32[]{:T(128)}, f32[]{:T(128)}) all-reduce(f32[]{:T(128)} %get-tuple-element.11, f32[]{:T(128)} %get-tuple-element.12), channel_id=1, replica_groups=mesh['row_0'=4,'row_1'=2,'col_0'=2,'col_1'=4,'col_2'=2] {'col_1'}, use_global_device_ids=true, to_apply=%region_4.0 | all-reduce | flops 2 | bytes 16 | tf_op jit(solution)/shard_map/psum | solution.py:14
  462.6 9.5 %all-reduce.3 = (f32[]{:T(128)}, f32[]{:T(128)}) all-reduce(f32[]{:T(128)} %get-tuple-element.5, f32[]{:T(128)} %get-tuple-element.6), channel_id=1, replica_groups=mesh['row_0'=4,'row_1'=2,'col_0'=2,'col_1'=4,'col_2'=2] {'col_2'}, use_global_device_ids=true, to_apply=%region_5.0 | all-reduce | flops 2 | bytes 16 | tf_op jit(solution)/shard_map/psum | solution.py:14
  473.6 0.1 add_multiply_fusion
  473.8 1.3 copy.50
  (15 shorter events, 0.5 us)
Async XLA Ops:
  6.5 276.2 %all-gather.2.cloned.1.call-start = ((), (), s32[]{:S(2)}) async-start(), calls=%async_computation.6 | async-start | bytes 17825792 | tf_op jit(solution)/shard_map/all_gather | solution.py:99
  41.7 5.1 %copy-start = (f32[2,128,1,128]{3,2,1,0:T(1,128)S(1)}, f32[2,128,1,128]{3,2,1,0:T(1,128)}, u32[]{:S(2)}) copy-start(f32[2,128,1,128]{3,2,1,0:T(1,128)} %param.7) | copy-start | bytes 393220
  41.7 162.1 %all-to-all-start = ((f32[8,2,128,7,128]{2,1,4,3,0:T(2,128)}), f32[8,2,128,7,128]{2,1,4,3,0:T(2,128)}, u32[]{:S(2)}, u32[]{:S(2)}) async-start(f32[8,2,128,7,128]{2,1,4,3,0:T(2,128)} %stack.2), calls=%async_computation | async-start | bytes 14680064 | tf_op jit(solution)/shard_map/all_to_all | solution.py:65
  46.7 330.2 %reduce-scatter.2.cloned.1.call-start = ((), (), s32[]{:S(2)}) async-start(), calls=%async_computation.5 | async-start | bytes 17825792 | tf_op jit(solution)/shard_map/reduce_scatter | solution.py:92
  414.9 58.6 %all-to-all-start.3 = ((f32[64,16,2,128]{3,2,0,1:T(2,128)}), f32[64,16,2,128]{3,2,0,1:T(2,128)S(1)}, u32[]{:S(2)}, u32[]{:S(2)}) async-start(f32[64,16,2,128]{3,2,0,1:T(2,128)} %copy.48), calls=%async_computation.4 | async-start | bytes 2097152 | tf_op jit(solution)/shard_map/all_to_all | solution.py:46
  422.2 13.2 %slice-start = ((f32[16,128,8,128]{3,2,1,0:T(8,128)}), f32[2,128,8,128]{3,2,1,0:T(8,128)S(1)}, s32[]{:S(2)}) async-start(f32[16,128,8,128]{3,2,1,0:T(8,128)} %param.5), calls=%async_computation.7 | async-start | bytes 2097152 | tf_op jit(solution)/shard_map/slice | solution.py:108
Sparse Core Ops, SparseCore 0:
  33.4 164.4 all-gather.1
  282.9 93.9 reduce-scatter.1
